TPU v7x, 32 devices: a whole 2x2x4 slice. The times are simulated.
32 devices in a mesh: wide: 16 (over z, y, x), narrow: 2 (over core).
Axes of the slice: x: 2, y: 2, z: 4, core: 2. Of those that a mesh axis runs over, the one named last changes fastest.
Arguments:
- contributions: float32 [2, 3, 8192, 128], P('narrow', None, 'wide'), may hold values from -6 to 6
- send_map: int32 [16, 800], P('wide'), may hold values from -1 to 511, as said below
- arrival_map: int32 [16, 800], P('wide'), may hold values from -1 to 255, as said below
- dual_diagonal: float32 [4096, 128], P('wide'), may hold values from 0.5 to 2
- mortar: bfloat16 [4096, 128, 128], P('wide'), may hold values from -0.5 to 0.5
- master_inverse: bfloat16 [4096, 128, 128], P('wide'), may hold values from -0.5 to 0.5
Outputs:
- corrections: float32 [2, 3, 8192, 128], P('narrow', None, 'wide')
Inputs may be any that keep to these rules, and one draw needn't show every extreme that they name: `send_map`: each row 0 to 511 of a partition stands in exactly one of its slots. Some stripe has all 50 of its slots used by every partition. arrival_map[d, o * 50 + c] is -1 exactly where send_map[o, d * 50 + c] is -1.
All inputs are finite; a program needn't handle non-finite values.
Results may differ from a plain program's by a relative error of at most 0.0041.
Values sent between devices are 32-bit elements; how exact they have to be, the bound alone decides.
No kernel may reach another device: no remote copies, remote signals or barrier semaphores. Data moves between devices by JAX's collectives and lax.ppermute only.
A program may use at most 64 MiB of HBM per device.

v0:
```python
import jax
import jax.numpy as jnp
from jax import lax
from jax.sharding import PartitionSpec as P


def partner_2(value, axis, stride):
    mask = 2**stride
    pairs = [(source, source ^ mask) for source in range(lax.axis_size(axis))]
    return lax.ppermute(value, axis, pairs)


def condense(slave_sums, master_sums, diagonal, mortar_part, inverse_part):
    multiplier_low = (slave_sums / diagonal[None]).astype(jnp.bfloat16)
    pushed = jnp.einsum(
        "bij,cbi->cbj", mortar_part, multiplier_low, preferred_element_type=jnp.float32
    )
    condensed_low = (master_sums + pushed).astype(jnp.bfloat16)
    master_fix = jnp.einsum(
        "bkj,cbj->cbk", inverse_part, condensed_low, preferred_element_type=jnp.float32
    )
    master_low = master_fix.astype(jnp.bfloat16)
    slave_fix = (
        jnp.einsum("bij,cbj->cbi", mortar_part, master_low, preferred_element_type=jnp.float32)
        / diagonal[None]
    )
    return (slave_fix, master_fix)


def shards(contributions, send_map, arrival_map, dual_diagonal, mortar, master_inverse):
    my_side = lax.axis_index("narrow")
    block_count = dual_diagonal.shape[0]
    node_count = contributions.shape[3]
    comp_count = contributions.shape[1]
    row_count = contributions.shape[2]
    picked = send_map[0]
    is_live = picked >= 0
    filled = jnp.where(is_live, picked, 0)
    outgoing = jnp.take(contributions[0], filled, axis=1) * is_live[None, :, None].astype(
        jnp.float32
    )
    landing = jnp.where(is_live, picked, row_count)
    block_ids = jnp.arange(block_count, dtype=jnp.int32)
    received_rows = lax.all_to_all(outgoing, "wide", split_axis=1, concat_axis=1, tiled=True)
    choosing_mask = (arrival_map[0][:, None] == block_ids[None, :]).astype(jnp.float32)
    local_row_sums = jnp.einsum(
        "gxp,xt->gtp", received_rows, choosing_mask, precision=lax.Precision.HIGHEST
    )
    partner = partner_2(local_row_sums, "narrow", 0)
    slave_sums = jnp.where(my_side == 0, local_row_sums, partner)
    master_sums = jnp.where(my_side == 0, partner, local_row_sums)
    slave_fix, master_fix = condense(slave_sums, master_sums, dual_diagonal, mortar, master_inverse)
    local_correction = jnp.where(my_side == 0, slave_fix, master_fix)
    departing_rows = jnp.einsum(
        "oxq,ux->ouq", local_correction, choosing_mask, precision=lax.Precision.HIGHEST
    )
    returned = lax.all_to_all(departing_rows, "wide", split_axis=1, concat_axis=1, tiled=True)
    placed = (
        jnp.zeros((comp_count, row_count + 1, node_count), jnp.float32)
        .at[:, landing, :]
        .set(returned)
    )
    return placed[:, :row_count][None]


def solution(mesh):
    placed = (
        P("narrow", None, "wide", None),
        P("wide", None),
        P("wide", None),
        P("wide", None),
        P("wide", None, None),
        P("wide", None, None),
    )
    return jax.shard_map(
        shards,
        mesh=mesh,
        in_specs=placed,
        out_specs=P("narrow", None, "wide", None),
        check_vma=False,
    )
```

profile of v0, /device:TPU:0, one launch (start us, length us, event | category | flops | bytes accessed | tf_op | source)
XLA Modules:
  0.0 153.0 jit_solution(14585886316772614351)
XLA Ops:
  0.0 0.7 fusion.21
  0.7 0.7 reduce.2
  1.5 1.7 %copy.37 = f32[1,3,512,128]{3,1,2,0:T(4,128)S(1)} copy(f32[1,3,512,128]{3,2,1,0:T(8,128)} %param.6) | data formatting | bytes 1572864 | tf_op args[0]
  3.1 3.6 %gather_fusion = f32[800,3,128]{2,1,0:T(4,128)S(1)} fusion(f32[3,512,128]{2,0,1:T(4,128)S(1)} %bitcast.35, s32[1024]{0:T(1024)S(1)} %pad_clamp_fusion), kind=kCustom, calls=%fused_computation | custom fusion | bytes 2460800 | tf_op jit(solution)/shard_map/jit(_take)/gather | solution.py:39
  6.8 5.0 %multiply_bitcast_fusion = f32[3,800,128]{2,0,1:T(4,128)} fusion(f32[800,3,128]{2,1,0:T(4,128)S(1)} %gather_fusion, f32[800]{0:T(1024)S(1)} %get-tuple-element.8, pred[800]{0:T(1024)(128)(4,1)S(1)} %get-tuple-element.7), kind=kLoop, calls=%fused_computation.2 | loop fusion | flops 614400 | bytes 2461600 | tf_op jit(solution)/shard_map/mul | solution.py:39
  11.8 8.5 %all-to-all-start = ((f32[3,800,128]{2,0,1:T(4,128)}), f32[3,800,128]{2,0,1:T(4,128)S(1)}, u32[]{:S(2)}, u32[]{:S(2)}) async-start(f32[3,800,128]{2,0,1:T(4,128)} %multiply_bitcast_fusion), calls=%async_computation | async-start | bytes 3276800 | tf_op jit(solution)/shard_map/all_to_all | solution.py:44
  20.3 0.0 copy-start
  20.3 35.2 %all-to-all-done = f32[3,800,128]{2,0,1:T(4,128)S(1)} async-done(((f32[3,800,128]{2,0,1:T(4,128)}), f32[3,800,128]{2,0,1:T(4,128)S(1)}, u32[]{:S(2)}, u32[]{:S(2)}) %all-to-all-start) | async-done | bytes 1228832 | tf_op jit(solution)/shard_map/all_to_all | solution.py:44
  55.5 1.2 fusion.4
  56.7 0.1 collective-permute-start
  56.8 1.7 %collective-permute-done = f32[3,256,128]{2,1,0:T(8,128)S(1)} collective-permute-done((f32[3,256,128]{2,1,0:T(8,128)S(1)}, f32[3,256,128]{2,1,0:T(8,128)S(1)}, u32[]{:S(2)}, u32[]{:S(2)}) %collective-permute-start) | collective-permute-done | bytes 393248 | tf_op jit(solution)/shard_map/ppermute | solution.py:10
  58.5 0.1 divide_convert_fusion
  58.5 0.0 slice-start
  58.5 5.8 %fusion.17 = f32[256,3,128]{2,1,0:T(4,128)S(1)} fusion(bf16[256,128,128]{2,1,0:T(8,128)(2,1)} %param.10, bf16[3,256,128]{2,1,0:T(8,128)(2,1)S(1)} %divide_convert_fusion), kind=kOutput, calls=%fused_computation.23 | convolution fusion | flops 25165824 | bytes 8978432 | tf_op jit(solution)/shard_map/bij,cbi->cbj/dot_general | solution.py:15
  64.3 0.1 fusion.12
  64.4 7.9 %fusion.15 = f32[256,3,128]{2,1,0:T(4,128)S(1)} fusion(bf16[256,128,128]{2,1,0:T(8,128)(2,1)} %param.11, bf16[3,256,128]{2,1,0:T(8,128)(2,1)S(1)} %fusion.12), kind=kOutput, calls=%fused_computation.21 | convolution fusion | flops 25165824 | bytes 8978432 | tf_op jit(solution)/shard_map/bkj,cbj->cbk/dot_general | solution.py:19
  72.4 4.4 %fusion.1 = f32[3,256,128]{2,0,1:T(4,128)S(1)} fusion(f32[256,3,128]{2,1,0:T(4,128)S(1)} %fusion.15, bf16[256,128,128]{2,1,0:T(8,128)(2,1)S(1)} %bitcast.33, f32[256,128]{1,0:T(8,128)S(1)} %copy-done, pred[]{:T(512)S(6)} %eq.24), kind=kOutput, calls=%fused_computation.6 | convolution fusion | flops 25460736 | bytes 9306113 | tf_op jit(solution)/shard_map/bij,cbj->cbi/dot_general | solution.py:24
  76.8 0.9 convolution_bitcast_fusion
  77.7 0.8 copy.23
  78.6 48.1 %all_to_all.10 = f32[3,800,128]{2,0,1:T(4,128)S(1)} all-to-all(f32[3,800,128]{2,0,1:T(4,128)S(1)} %copy.23), channel_id=1, replica_groups=mesh['wide'=16,'narrow'=2] {'wide'}, dimensions={1} | all-to-all | bytes 2457600 | tf_op jit(solution)/shard_map/all_to_all | solution.py:57
  126.6 0.1 broadcast_in_dim.28
  126.8 25.1 %scatter_fusion = f32[3,513,128]{2,0,1:T(4,128)S(1)} fusion(f32[3,513,128]{2,0,1:T(4,128)S(1)} %broadcast_in_dim.28, s32[800]{0:T(1024)S(1)} %get-tuple-element.6, f32[800,3,128]{2,1,0:T(4,128)S(1)} %bitcast.34), kind=kCustom, calls=%fused_computation.1 | custom fusion | bytes 3689600 | tf_op jit(solution)/shard_map/scatter | solution.py:61
  151.9 0.2 slice_bitcast_fusion
  152.1 0.9 copy.24
  (10 shorter events, 0.0 us)
Async XLA Ops:
  11.8 8.5 %copy-start.1 = (s32[1,800]{1,0:T(1,128)S(1)}, s32[1,800]{1,0:T(1,128)}, u32[]{:S(2)}) copy-start(s32[1,800]{1,0:T(1,128)} %param.8) | copy-start | bytes 9604
  11.8 43.7 %all-to-all-start = ((f32[3,800,128]{2,0,1:T(4,128)}), f32[3,800,128]{2,0,1:T(4,128)S(1)}, u32[]{:S(2)}, u32[]{:S(2)}) async-start(f32[3,800,128]{2,0,1:T(4,128)} %multiply_bitcast_fusion), calls=%async_computation | async-start | bytes 3276800 | tf_op jit(solution)/shard_map/all_to_all | solution.py:44
  20.3 38.2 %copy-start = (f32[256,128]{1,0:T(8,128)S(1)}, f32[256,128]{1,0:T(8,128)}, u32[]{:S(2)}) copy-start(f32[256,128]{1,0:T(8,128)} %param.9) | copy-start | bytes 393220
  56.7 1.8 %collective-permute-start = (f32[3,256,128]{2,1,0:T(8,128)S(1)}, f32[3,256,128]{2,1,0:T(8,128)S(1)}, u32[]{:S(2)}, u32[]{:S(2)}) collective-permute-start(f32[3,256,128]{2,1,0:T(8,128)S(1)} %fusion.4), channel_id=1, source_target_pairs={{0,1},{1,0},{2,3},{3,2},{4,5},{5,4},{6,7},{7,6},{8,9},{9,8},{10,11... | collective-permute-start | bytes 1179656 | tf_op jit(solution)/shard_map/ppermute | solution.py:10
  58.5 13.8 %slice-start = ((s8[8388608]{0:T(1024)(128)(4,1)}), s8[4194304]{0:T(1024)(128)(4,1)S(1)}, s32[]{:S(2)}) async-start(s8[8388608]{0:T(1024)(128)(4,1)} %bitcast.32), calls=%async_computation.2 | async-start | bytes 8388608
  64.3 8.0 %slice-start.1 = ((s8[8388608]{0:T(1024)(128)(4,1)}), s8[4194304]{0:T(1024)(128)(4,1)S(1)}, s32[]{:S(2)}) async-start(s8[8388608]{0:T(1024)(128)(4,1)} %bitcast.32), calls=%async_computation.3 | async-start | bytes 8388608
where the time goes:
time: 153 us
  blocking collectives  48.1 us (31%)
  waiting for transfers between devices  36.9 us (24%)
  local copies, waits for them, and re-layouts  32.5 us (21%)
  matrix products  20.3 us (13%)
  starting transfers between devices  8.54 us (6%)
  other arithmetic  6.57 us (4%)
    all_to_all x1, blocking collectives, shards(): lax.all_to_all(departing_rows, 'wide', split_axis=1, concat_axis=1, tiled...  48.1 us
    all_to_all x1, waiting for transfers between devices, shards(): lax.all_to_all(outgoing, 'wide', split_axis=1, concat_axis=1, tiled=True)  35.2 us
    scatter x1, local copies, waits for them, and re-layouts, shards(): placed = jnp.zeros((comp_count, row_count + 1, node_count), jnp.float32)....  25.1 us
    all_to_all x1, starting transfers between devices, shards(): lax.all_to_all(outgoing, 'wide', split_axis=1, concat_axis=1, tiled=True)  8.47 us
    dot_general x1, matrix products, condense(): jnp.einsum('bkj,cbj->cbk', inverse_part, condensed_low, preferred_element...  7.93 us
    dot_general x1, matrix products, condense(): jnp.einsum('bij,cbi->cbj', mortar_part, multiplier_low, preferred_element...  5.8 us
    mul x1, other arithmetic, shards(): jnp.take(contributions[0], filled, axis=1)  4.99 us
    dot_general x1, matrix products, condense(): jnp.einsum('bij,cbj->cbi', mortar_part, master_low, preferred_element_typ...  4.45 us
  transfers between devices with their start and end apart: 2, of which 2 were waited for; matrix products, arithmetic and copies ran while one was open for 0% of the time, Pallas kernels for 0%

commit v1 on v0

v1 whole, which is shorter than its diff:
```python
import functools

import jax
import jax.numpy as jnp
from jax import lax
from jax.experimental import pallas as pl
from jax.experimental.pallas import tpu as pltpu
from jax.sharding import PartitionSpec as P


VMEM = pltpu.VMEM
SMEM = pltpu.SMEM


def distance_plan(wide):
    half, quarter = wide // 2, wide // 4
    upper = list(range(half + quarter, wide))
    lower = list(range(half + 1, half + quarter))
    pairs = list(zip(upper, lower))
    pairs.append((upper[-1], quarter))
    near = [d for d in range(1, half) if d != quarter]
    pairs += list(zip(near[0::2], near[1::2]))
    return half, pairs


def hop_both(value, wide, distance):
    return lax.ppermute(value, "wide", [(i, i ^ distance) for i in range(wide)])


def hop_split(value, wide, pair):
    links = [(2 * i + core, 2 * (i ^ pair[core]) + core) for i in range(wide) for core in (0, 1)]
    return lax.ppermute(value, ("wide", "narrow"), links)


def swap_cores(value):
    return lax.ppermute(value, "narrow", [(0, 1), (1, 0)])


def copy_rows(source, target, index_of, count, offset, comps, nodes):
    for slot in range(count):
        row = index_of(slot)
        for c in range(comps):
            target[offset + slot : offset + slot + 1, c * nodes : (c + 1) * nodes] = source[
                c, pl.ds(row, 1), :
            ]


def gather_near(cap, half, place, send, own, far_out, home_out):
    comps, nodes = own.shape[0], own.shape[2]
    for out, distance in ((far_out, half), (home_out, 0)):
        base = (place[0] ^ distance) * cap
        copy_rows(own, out, lambda s: jnp.maximum(send[base + s], 0), cap, 0, comps, nodes)


def gather_pairs(cap, pairs, place, send, own, other, *outs):
    comps, nodes = own.shape[0], own.shape[2]
    for (first, second), out in zip(pairs, outs):
        base = (place[0] ^ jnp.where(place[1] == 0, first, second)) * cap
        index_of = lambda s: jnp.maximum(send[base + s], 0)
        copy_rows(own, out, index_of, cap, 0, comps, nodes)
        copy_rows(other, out, index_of, cap, cap, comps, nodes)


def add_rows(cap, half, pairs, place, spots, *refs):
    doubles, far, home, keep, give = refs[: len(pairs)], *refs[len(pairs) :]
    spot_count = keep.shape[0] + give.shape[0]
    total = None

    def add(total, rows, ids):
        count = rows.shape[0]
        hot = lax.broadcasted_iota(jnp.int32, (spot_count, count), 0) == ids
        hot = hot.astype(jnp.float32).astype(jnp.bfloat16)
        high = rows.astype(jnp.bfloat16)
        low = (rows - high.astype(jnp.float32)).astype(jnp.bfloat16)
        for part in (high, low):
            piece = jnp.dot(hot, part, preferred_element_type=jnp.float32)
            total = piece if total is None else total + piece
        return total

    for (first, second), ref in zip(pairs, doubles):
        source = place[0] ^ jnp.where(place[1] == 0, first, second)
        total = add(total, ref[...], spots[pl.ds(source, 1), :])
    for ref, distance in ((far, half), (home, 0)):
        total = add(total, ref[...], spots[pl.ds(place[0] ^ distance, 1), :cap])
    keep[...] = total[: keep.shape[0]]
    give[...] = total[keep.shape[0] :]


def solve(group, comps, place, keep, got, diagonal, mortar, inverse, out):
    nodes = diagonal.shape[1]
    blocks = diagonal.shape[0]
    row = lax.broadcasted_iota(jnp.int32, (comps * group, nodes), 0) % group

    def stage(stacked, matrix, contract):
        picked = None
        for g in range(group):
            full = lax.dot_general(
                stacked, matrix(g), (((1,), (contract,)), ((), ())), preferred_element_type=jnp.float32
            )
            picked = full if picked is None else jnp.where(row == g, full, picked)
        return picked

    def stack(value):
        return jnp.concatenate([value[:, c * nodes : (c + 1) * nodes] for c in range(comps)], axis=0)

    for start in range(0, blocks, group):
        here = pl.ds(start, group)
        scale = jnp.concatenate([diagonal[here, :]] * comps, axis=0)
        slave = stack(keep[0, here, :] + got[0, here, :])
        master = stack(keep[1, here, :] + got[1, here, :])
        multiplier = (slave / scale).astype(jnp.bfloat16)
        condensed = master + stage(multiplier, lambda g: mortar[start + g], 0)
        fix = stage(condensed.astype(jnp.bfloat16), lambda g: inverse[start + g], 1)
        back = stage(fix.astype(jnp.bfloat16), lambda g: mortar[start + g], 1) / scale
        for c in range(comps):
            lanes = slice(c * nodes, (c + 1) * nodes)
            out[0, here, lanes] = back[c * group : (c + 1) * group]
            out[1, here, lanes] = fix[c * group : (c + 1) * group]


def spread_rows(cap, half, pairs, place, spots, keep, got, *refs):
    outs, far, home, table = refs[: len(pairs)], *refs[len(pairs) :]
    side = keep.shape[0]
    table[:side] = keep[...]
    table[side:] = got[...]

    def copy(out, source, count):
        for s in range(count):
            spot = jnp.maximum(spots[source, s], 0)
            out[s : s + 1, :] = table[pl.ds(spot, 1), :]

    for (first, second), out in zip(pairs, outs):
        copy(out, place[0] ^ jnp.where(place[1] == 0, first, second), 2 * cap)
    copy(far, place[0] ^ half, cap)
    copy(home, place[0], cap)


def split_other(cap, pairs, *refs):
    doubles, out = refs[: len(pairs)], refs[len(pairs)]
    for k, ref in enumerate(doubles):
        out[k] = ref[cap:, :]


def place_rows(cap, half, pairs, place, send, swapped, *refs):
    doubles, far, home, out = refs[: len(pairs)], *refs[len(pairs) :]
    comps, _, nodes = out.shape

    def put(source, base, read):
        for s in range(cap):
            row = send[base + s]

            @pl.when(row >= 0)
            def _():
                for c in range(comps):
                    out[c, pl.ds(row, 1), :] = read(source, s, slice(c * nodes, (c + 1) * nodes))

    plain = lambda ref, s, lanes: ref[s : s + 1, lanes]
    for k, ((first, second), ref) in enumerate(zip(pairs, doubles)):
        mine = place[0] ^ jnp.where(place[1] == 0, first, second)
        theirs = place[0] ^ jnp.where(place[1] == 0, second, first)
        put(ref, mine * cap, plain)
        put(swapped, theirs * cap, lambda ref, s, lanes: ref[k, s : s + 1, lanes])
    put(far, (place[0] ^ half) * cap, plain)
    put(home, place[0] * cap, plain)


def call(body, outs, args, spaces, scratch=()):
    return pl.pallas_call(
        body,
        out_shape=outs,
        in_specs=[pl.BlockSpec(memory_space=s) for s in spaces],
        out_specs=jax.tree.map(lambda _: pl.BlockSpec(memory_space=VMEM), outs),
        scratch_shapes=scratch,
    )(*args)


def shards(wide, contributions, send_map, arrival_map, dual_diagonal, mortar, master_inverse):
    half, pairs = distance_plan(wide)
    comps, rows, nodes = contributions.shape[1:]
    blocks = dual_diagonal.shape[0]
    cap = send_map.shape[1] // wide
    part = blocks // 2
    core = lax.axis_index("narrow")
    place = jnp.stack([lax.axis_index("wide"), core]).astype(jnp.int32)
    f32 = lambda *shape: jax.ShapeDtypeStruct(shape, jnp.float32)
    single, double = f32(cap, comps * nodes), f32(2 * cap, comps * nodes)
    count = len(pairs)

    own = contributions[0]
    send = send_map[0]
    other = swap_cores(own)

    block = arrival_map[0].reshape(wide, cap)
    low = block % part + jnp.where(block // part == core, 0, 2 * part)
    spot = lambda side: jnp.where(block < 0, -1, low + side * part)
    spots = jnp.concatenate([spot(core), spot(1 - core)], axis=1)

    far_row, home_row = call(
        functools.partial(gather_near, cap, half),
        [single, single],
        (place, send, own),
        (SMEM, SMEM, VMEM),
    )
    far_row = hop_both(far_row, wide, half)
    sent = call(
        functools.partial(gather_pairs, cap, pairs),
        [double] * count,
        (place, send, own, other),
        (SMEM, SMEM, VMEM, VMEM),
    )
    came = []
    for k, pair in enumerate(pairs):
        came.append(hop_split(sent[k], wide, pair))

    keep, give = call(
        functools.partial(add_rows, cap, half, pairs),
        [f32(2 * part, comps * nodes)] * 2,
        (place, spots, *came, far_row, home_row),
        (SMEM, VMEM) + (VMEM,) * (count + 2),
    )
    got = swap_cores(give)

    steps = 4
    step = part // steps
    table = (2, part, comps * nodes)
    offset = lambda i, place: (place[1] * steps + i, 0, 0)
    fixes = pl.pallas_call(
        functools.partial(solve, 8, comps),
        out_shape=f32(*table),
        grid_spec=pltpu.PrefetchScalarGridSpec(
            num_scalar_prefetch=1,
            grid=(steps,),
            in_specs=[
                pl.BlockSpec((2, step, comps * nodes), lambda i, place: (0, i, 0)),
                pl.BlockSpec((2, step, comps * nodes), lambda i, place: (0, i, 0)),
                pl.BlockSpec((step, nodes), lambda i, place: (place[1] * steps + i, 0)),
                pl.BlockSpec((step, nodes, nodes), offset),
                pl.BlockSpec((step, nodes, nodes), offset),
            ],
            out_specs=pl.BlockSpec((2, step, comps * nodes), lambda i, place: (0, i, 0)),
        ),
        name="solve",
    )(place, keep.reshape(table), got.reshape(table), dual_diagonal, mortar, master_inverse)
    fixes = fixes.reshape(2 * part, comps * nodes)
    got_fixes = swap_cores(fixes)

    *sent, far_row, home_row = call(
        functools.partial(spread_rows, cap, half, pairs),
        [double] * count + [single, single],
        (place, spots, fixes, got_fixes),
        (SMEM, SMEM, VMEM, VMEM),
        scratch=[VMEM((4 * part, comps * nodes), jnp.float32)],
    )
    came = []
    for k, pair in enumerate(pairs):
        came.append(hop_split(sent[k], wide, pair))
    far_row = hop_both(far_row, wide, half)

    theirs = call(
        functools.partial(split_other, cap, pairs),
        f32(count, cap, comps * nodes),
        came,
        (VMEM,) * count,
    )
    swapped = swap_cores(theirs)
    placed = call(
        functools.partial(place_rows, cap, half, pairs),
        f32(comps, rows, nodes),
        (place, send, swapped, *came, far_row, home_row),
        (SMEM, SMEM) + (VMEM,) * (count + 3),
    )
    return placed[None]


def solution(mesh):
    wide = mesh.shape["wide"]
    _, _ = distance_plan(wide)

    def step(*args):
        return shards(wide, *args)

    placed = (
        P("narrow", None, "wide", None),
        P("wide", None),
        P("wide", None),
        P("wide", None),
        P("wide", None, None),
        P("wide", None, None),
    )
    return jax.shard_map(
        step,
        mesh=mesh,
        in_specs=placed,
        out_specs=P("narrow", None, "wide", None),
        check_vma=False,
    )
```

time: 153 us -> 126 us (0.82)
  blocking collectives: 48.1 us -> 0 us
  Pallas kernels: 0 us -> 36.2 us
  starting transfers between devices: 8.54 us -> 44.1 us
  local copies, waits for them, and re-layouts: 32.5 us -> 4.68 us
  matrix products: 20.3 us -> 0 us
  other arithmetic: 6.57 us -> 3.27 us
    all_to_all x1 -> x0, blocking collectives: 48.1 us -> none  [shards(): lax.all_to_all(departing_rows, 'wide', split_axis=1, concat_axis=1, tiled...]
    ppermute x1 -> x20, starting transfers between devices: 0.07 us -> 44.1 us  [the longest x14 37.9 us: hop_split(): return lax.ppermute(value, ('wide', 'narrow'), links)]
    pallas_call x0 -> x7, Pallas kernels: none -> 36.2 us  [the longest x6 24.6 us: call(): pl.pallas_call(body, out_shape=outs, in_specs=[pl.BlockSpec(memory_space=...]
    ppermute x1 -> x20, waiting for transfers between devices: 1.7 us -> 37.3 us  [the longest x2 19.5 us: hop_both(): return lax.ppermute(value, 'wide', [(i, i ^ distance) for i in range(wide)])]
    all_to_all x1 -> x0, waiting for transfers between devices: 35.2 us -> none  [shards(): lax.all_to_all(outgoing, 'wide', split_axis=1, concat_axis=1, tiled=True)]
    scatter x1 -> x0, local copies, waits for them, and re-layouts: 25.1 us -> none  [shards(): placed = jnp.zeros((comp_count, row_count + 1, node_count), jnp.float32)....]
    dot_general x5 -> x0, matrix products: 20.3 us -> none  [the longest x1 7.93 us: condense(): jnp.einsum('bkj,cbj->cbk', inverse_part, condensed_low, preferred_element...]
    all_to_all x1 -> x0, starting transfers between devices: 8.47 us -> none  [shards(): lax.all_to_all(outgoing, 'wide', split_axis=1, concat_axis=1, tiled=True)]
  transfers between devices with their start and end apart: 2 -> 20, of which waited for: 2 -> 9; matrix products, arithmetic and copies ran while one was open for 0% -> 3% of each run, Pallas kernels for 0% -> 2%
where the time goes in v1:
time: 126 us
  starting transfers between devices  44.1 us (35%)
  waiting for transfers between devices  37.3 us (30%)
  Pallas kernels  36.2 us (29%)
  local copies, waits for them, and re-layouts  4.68 us (4%)
  other arithmetic  3.27 us (3%)
    ppermute x14, starting transfers between devices, hop_split(): return lax.ppermute(value, ('wide', 'narrow'), links)  37.9 us
    pallas_call x6, Pallas kernels, call(): pl.pallas_call(body, out_shape=outs, in_specs=[pl.BlockSpec(memory_space=...  24.6 us
    ppermute x2, waiting for transfers between devices, hop_both(): return lax.ppermute(value, 'wide', [(i, i ^ distance) for i in range(wide)])  19.5 us
    ppermute x14, waiting for transfers between devices, hop_split(): return lax.ppermute(value, ('wide', 'narrow'), links)  13.9 us
    pallas_call x1, Pallas kernels, shards(): pl.pallas_call(functools.partial(solve, 8, comps), out_shape=f32(*table),...  11.7 us
    unnamed x40, local copies, waits for them, and re-layouts  4.6 us
    ppermute x2, starting transfers between devices, hop_both(): return lax.ppermute(value, 'wide', [(i, i ^ distance) for i in range(wide)])  4.15 us
    ppermute x4, waiting for transfers between devices, swap_cores(): return lax.ppermute(value, 'narrow', [(0, 1), (1, 0)])  3.97 us
  transfers between devices with their start and end apart: 20, of which 9 were waited for; matrix products, arithmetic and copies ran while one was open for 3% of the time, Pallas kernels for 2%

profile of v1, /device:TPU:0, one launch (start us, length us, event | category | flops | bytes accessed | tf_op | source)
XLA Modules:
  0.0 125.8 jit_solution(5831154611887914915)
XLA Ops:
  3.5 3.5 %shard_map.64 = (f32[100,384]{1,0:T(8,128)}, f32[100,384]{1,0:T(8,128)}, f32[100,384]{1,0:T(8,128)}, f32[100,384]{1,0:T(8,128)}, f32[100,384]{1,0:T(8,128)}, /*index=5*/f32[100,384]{1,0:T(8,128)}, f32[100,384]{1,0:T(8,128)}) custom-call(s32[2]{0:T(128)} %pad_add_fusion.1.place, s32[800]{0:T(1024)} %reduce.send, f32[3,512,128]{2,1,0:T(8,128)} %bitcast.8, ...), custom_call_target="tpu_custom_call" | custom-call | tf_op jit(solution)/shard_map/pallas_call | solution.py:168
  7.0 5.0 %collective-permute-start.1 = (f32[100,384]{1,0:T(8,128)}, f32[100,384]{1,0:T(8,128)S(1)}, u32[]{:S(2)}, u32[]{:S(2)}) collective-permute-start(f32[100,384]{1,0:T(8,128)} %get-tuple-element.25), channel_id=1, source_target_pairs={{0,24},{1,19},{2,26},{3,17},{4,28},{5,23},{6,30},{7,21},{8,16},{9,... | collective-permute-start | bytes 460808 | tf_op jit(solution)/shard_map/ppermute | solution.py:32
  13.1 2.0 %shard_map.65 = (f32[50,384]{1,0:T(8,128)}, f32[50,384]{1,0:T(8,128)}) custom-call(s32[2]{0:T(128)} %pad_add_fusion.1.place, s32[800]{0:T(1024)} %reduce.send, f32[3,512,128]{2,1,0:T(8,128)} %bitcast.9), custom_call_target="tpu_custom_call" | custom-call | tf_op jit(solution)/shard_map/pallas_call | solution.py:168
  16.7 3.8 %collective-permute-start.3 = (f32[100,384]{1,0:T(8,128)}, f32[100,384]{1,0:T(8,128)S(1)}, u32[]{:S(2)}, u32[]{:S(2)}) collective-permute-start(f32[100,384]{1,0:T(8,128)} %get-tuple-element.27), channel_id=1, source_target_pairs={{0,28},{1,23},{2,30},{3,21},{4,24},{5,19},{6,26},{7,17},{8,20},{9,... | collective-permute-start | bytes 460808 | tf_op jit(solution)/shard_map/ppermute | solution.py:32
  21.5 14.2 %collective-permute-done.8.refs_7_ = f32[50,384]{1,0:T(8,128)S(1)} collective-permute-done((f32[50,384]{1,0:T(8,128)}, f32[50,384]{1,0:T(8,128)S(1)}, u32[]{:S(2)}, u32[]{:S(2)}) %collective-permute-start.8) | collective-permute-done | bytes 76832 | tf_op jit(solution)/shard_map/ppermute | solution.py:27
  35.7 1.5 %collective-permute-start.5 = (f32[100,384]{1,0:T(8,128)}, f32[100,384]{1,0:T(8,128)S(1)}, u32[]{:S(2)}, u32[]{:S(2)}) collective-permute-start(f32[100,384]{1,0:T(8,128)} %get-tuple-element.29), channel_id=1, source_target_pairs={{0,2},{1,5},{2,0},{3,7},{4,6},{5,1},{6,4},{7,3},{8,10},{9,13},{10,... | collective-permute-start | bytes 460808 | tf_op jit(solution)/shard_map/ppermute | solution.py:32
  37.2 1.5 %collective-permute-start.6 = (f32[100,384]{1,0:T(8,128)}, f32[100,384]{1,0:T(8,128)S(1)}, u32[]{:S(2)}, u32[]{:S(2)}) collective-permute-start(f32[100,384]{1,0:T(8,128)} %get-tuple-element.30), channel_id=1, source_target_pairs={{0,6},{1,11},{2,4},{3,9},{4,2},{5,15},{6,0},{7,13},{8,14},{9,3},{1... | collective-permute-start | bytes 460808 | tf_op jit(solution)/shard_map/ppermute | solution.py:32
  39.4 4.7 %collective-permute-done.5.refs_4_ = f32[100,384]{1,0:T(8,128)S(1)} collective-permute-done((f32[100,384]{1,0:T(8,128)}, f32[100,384]{1,0:T(8,128)S(1)}, u32[]{:S(2)}, u32[]{:S(2)}) %collective-permute-start.5) | collective-permute-done | bytes 153632 | tf_op jit(solution)/shard_map/ppermute | solution.py:32
  44.2 3.5 %collective-permute-done.6.refs_5_ = f32[100,384]{1,0:T(8,128)S(1)} collective-permute-done((f32[100,384]{1,0:T(8,128)}, f32[100,384]{1,0:T(8,128)S(1)}, u32[]{:S(2)}, u32[]{:S(2)}) %collective-permute-start.6) | collective-permute-done | bytes 153632 | tf_op jit(solution)/shard_map/ppermute | solution.py:32
  48.3 4.2 %shard_map.66 = (f32[256,384]{1,0:T(8,128)}, f32[256,384]{1,0:T(8,128)}) custom-call(s32[2]{0:T(128)} %pad_add_fusion.1.place, s32[16,100]{1,0:T(8,128)} %pad_add_fusion.spots, f32[100,384]{1,0:T(8,128)} %copy-done.11, f32[100,384]{1,0:T(8,128)} %copy-done.12, f32[100,384]{1,0:T(8,128)} %copy-done.13, f32[100,384]{1,0:T(8,128)} %copy-done.14, ...), custom_call_target="tpu_custom_call" | custom-call | tf_op jit(solution)/shard_map/pallas_call | solution.py:168
  52.6 1.9 %collective-permute-done.9 = f32[256,384]{1,0:T(8,128)S(1)} collective-permute-done((f32[256,384]{1,0:T(8,128)}, f32[256,384]{1,0:T(8,128)S(1)}, u32[]{:S(2)}, u32[]{:S(2)}) %collective-permute-start.9) | collective-permute-done | bytes 393248 | tf_op jit(solution)/shard_map/ppermute | solution.py:36
  55.2 11.7 %solve.1 = f32[2,128,384]{2,1,0:T(8,128)} custom-call(s32[2]{0:T(128)} %pad_add_fusion.1.place, f32[2,128,384]{2,1,0:T(8,128)} %bitcast.12, f32[2,128,384]{2,1,0:T(8,128)} %bitcast.13, f32[256,128]{1,0:T(8,128)} %diagonal.1, bf16[256,128,128]{2,1,0:T(8,128)(2,1)} %mortar.1, bf16[256,128,128]{2,1,0:T(8,128)(2,1)} %inverse.1), custom_call_target="tpu_custom_call" | custom-call | tf_op jit(solution)/shard_map/solve/pallas_call | solution.py:227
  67.0 1.8 %collective-permute-done.10.got = f32[256,384]{1,0:T(8,128)S(1)} collective-permute-done((f32[256,384]{1,0:T(8,128)}, f32[256,384]{1,0:T(8,128)S(1)}, u32[]{:S(2)}, u32[]{:S(2)}) %collective-permute-start.10) | collective-permute-done | bytes 393248 | tf_op jit(solution)/shard_map/ppermute | solution.py:36
  69.6 4.1 %shard_map.67 = (f32[100,384]{1,0:T(8,128)}, f32[100,384]{1,0:T(8,128)}, f32[100,384]{1,0:T(8,128)}, f32[100,384]{1,0:T(8,128)}, f32[100,384]{1,0:T(8,128)}, /*i...) custom-call(s32[2]{0:T(128)} %pad_add_fusion.1.place, ...), custom_call_target="tpu_custom_call" | custom-call | tf_op jit(solution)/shard_map/pallas_call | solution.py:168
  73.6 3.0 %collective-permute-start.11 = (f32[100,384]{1,0:T(8,128)}, f32[100,384]{1,0:T(8,128)S(1)}, u32[]{:S(2)}, u32[]{:S(2)}) collective-permute-start(f32[100,384]{1,0:T(8,128)} %get-tuple-element.36), channel_id=1, source_target_pairs={{0,24},{1,19},{2,26},{3,17},{4,28},{5,23},{6,30},{7,21},{8,16},{9,... | collective-permute-start | bytes 460808 | tf_op jit(solution)/shard_map/ppermute | solution.py:32
  76.7 1.5 %collective-permute-start.12 = (f32[100,384]{1,0:T(8,128)}, f32[100,384]{1,0:T(8,128)S(1)}, u32[]{:S(2)}, u32[]{:S(2)}) collective-permute-start(f32[100,384]{1,0:T(8,128)} %get-tuple-element.37), channel_id=1, source_target_pairs={{0,26},{1,21},{2,24},{3,23},{4,30},{5,17},{6,28},{7,19},{8,18},{9,... | collective-permute-start | bytes 460808 | tf_op jit(solution)/shard_map/ppermute | solution.py:32
  78.2 3.7 %collective-permute-start.13 = (f32[100,384]{1,0:T(8,128)}, f32[100,384]{1,0:T(8,128)S(1)}, u32[]{:S(2)}, u32[]{:S(2)}) collective-permute-start(f32[100,384]{1,0:T(8,128)} %get-tuple-element.38), channel_id=1, source_target_pairs={{0,28},{1,23},{2,30},{3,21},{4,24},{5,19},{6,26},{7,17},{8,20},{9,... | collective-permute-start | bytes 460808 | tf_op jit(solution)/shard_map/ppermute | solution.py:32
  84.4 1.6 %collective-permute-start.16 = (f32[100,384]{1,0:T(8,128)}, f32[100,384]{1,0:T(8,128)S(1)}, u32[]{:S(2)}, u32[]{:S(2)}) collective-permute-start(f32[100,384]{1,0:T(8,128)} %get-tuple-element.41), channel_id=1, source_target_pairs={{0,6},{1,11},{2,4},{3,9},{4,2},{5,15},{6,0},{7,13},{8,14},{9,3},{1... | collective-permute-start | bytes 460808 | tf_op jit(solution)/shard_map/ppermute | solution.py:32
  86.6 11.7 %collective-permute-start.17 = (f32[100,384]{1,0:T(8,128)}, f32[100,384]{1,0:T(8,128)S(1)}, u32[]{:S(2)}, u32[]{:S(2)}) collective-permute-start(f32[100,384]{1,0:T(8,128)} %get-tuple-element.42), channel_id=1, source_target_pairs={{0,12},{1,15},{2,14},{3,13},{4,8},{5,11},{6,10},{7,9},{8,4},{9,7},... | collective-permute-start | bytes 460808 | tf_op jit(solution)/shard_map/ppermute | solution.py:32
  98.4 5.1 %collective-permute-done.17.refs_6_ = f32[100,384]{1,0:T(8,128)S(1)} collective-permute-done((f32[100,384]{1,0:T(8,128)}, f32[100,384]{1,0:T(8,128)S(1)}, u32[]{:S(2)}, u32[]{:S(2)}) %collective-permute-start.17) | collective-permute-done | bytes 153632 | tf_op jit(solution)/shard_map/ppermute | solution.py:32
  104.1 2.2 %shard_map.68 = f32[7,50,384]{2,1,0:T(8,128)} custom-call(f32[100,384]{1,0:T(8,128)} %copy-done.1, f32[100,384]{1,0:T(8,128)} %copy-done.2, f32[100,384]{1,0:T(8,128)} %copy-done.3, f32[100,384]{1,0:T(8,128)} %copy-done.4, f32[100,384]{1,0:T(8,128)} %copy-done.5, f32[100,384]{1,0:T(8,128)} %copy-done.6, f32[100,384]{1,0:T(8,128)} %copy-done.7), custom_call_target="tpu_custom_call" | custom-call | tf_op jit(solution)/shard_map/pallas_call | solution.py:168
  107.7 3.4 %collective-permute-start.19 = (f32[50,384]{1,0:T(8,128)}, f32[50,384]{1,0:T(8,128)S(1)}, u32[]{:S(2)}, u32[]{:S(2)}) collective-permute-start(f32[50,384]{1,0:T(8,128)} %get-tuple-element.43), channel_id=1, source_target_pairs={{0,16},{2,18},{4,20},{6,22},{8,24},{10,26},{12,28},{14,30},{16,0},... | collective-permute-start | bytes 230408 | tf_op jit(solution)/shard_map/ppermute | solution.py:27
  111.1 5.3 %collective-permute-done.19.refs_7_ = f32[50,384]{1,0:T(8,128)S(1)} collective-permute-done((f32[50,384]{1,0:T(8,128)}, f32[50,384]{1,0:T(8,128)S(1)}, u32[]{:S(2)}, u32[]{:S(2)}) %collective-permute-start.19) | collective-permute-done | bytes 76832 | tf_op jit(solution)/shard_map/ppermute | solution.py:27
  117.2 8.6 %shard_map.69 = f32[3,512,128]{2,1,0:T(8,128)} custom-call(s32[2]{0:T(128)} %pad_add_fusion.1.place, s32[800]{0:T(1024)} %reduce.send, f32[7,50,384]{2,1,0:T(8,128)} %copy-done.8, f32[100,384]{1,0:T(8,128)} %copy-done.1, f32[100,384]{1,0:T(8,128)} %copy-done.2, f32[100,384]{1,0:T(8,128)} %copy-done.3, f32[100,384]{1,0:T(8,128)} %copy-done.4, ...), custom_call_target="tpu_custom_call" | custom-call | tf_op jit(solution)/shard_map/pallas_call | solution.py:168
  (69 shorter events, 16.2 us)
Async XLA Ops:
  0.0 2.6 %collective-permute-start = (f32[3,512,128]{2,1,0:T(8,128)}, f32[3,512,128]{2,1,0:T(8,128)S(1)}, u32[]{:S(2)}, u32[]{:S(2)}) collective-permute-start(f32[3,512,128]{2,1,0:T(8,128)} %bitcast.7), channel_id=1, source_target_pairs={{0,1},{1,0},{2,3},{3,2},{4,5},{5,4},{6,7},{7,6},{8,9},{9,8},{10,11... | collective-permute-start | bytes 2359304 | tf_op jit(solution)/shard_map/ppermute | solution.py:36
  7.0 30.2 %collective-permute-start.1 = (f32[100,384]{1,0:T(8,128)}, f32[100,384]{1,0:T(8,128)S(1)}, u32[]{:S(2)}, u32[]{:S(2)}) collective-permute-start(f32[100,384]{1,0:T(8,128)} %get-tuple-element.25), channel_id=1, source_target_pairs={{0,24},{1,19},{2,26},{3,17},{4,28},{5,23},{6,30},{7,21},{8,16},{9,... | collective-permute-start | bytes 460808 | tf_op jit(solution)/shard_map/ppermute | solution.py:32
  12.0 26.7 %collective-permute-start.2 = (f32[100,384]{1,0:T(8,128)}, f32[100,384]{1,0:T(8,128)S(1)}, u32[]{:S(2)}, u32[]{:S(2)}) collective-permute-start(f32[100,384]{1,0:T(8,128)} %get-tuple-element.26), channel_id=1, source_target_pairs={{0,26},{1,21},{2,24},{3,23},{4,30},{5,17},{6,28},{7,19},{8,18},{9,... | collective-permute-start | bytes 460808 | tf_op jit(solution)/shard_map/ppermute | solution.py:32
  15.1 20.6 %collective-permute-start.8 = (f32[50,384]{1,0:T(8,128)}, f32[50,384]{1,0:T(8,128)S(1)}, u32[]{:S(2)}, u32[]{:S(2)}) collective-permute-start(f32[50,384]{1,0:T(8,128)} %get-tuple-element.32), channel_id=1, source_target_pairs={{0,16},{2,18},{4,20},{6,22},{8,24},{10,26},{12,28},{14,30},{16,0},... | collective-permute-start | bytes 230408 | tf_op jit(solution)/shard_map/ppermute | solution.py:27
  16.7 22.7 %collective-permute-start.3 = (f32[100,384]{1,0:T(8,128)}, f32[100,384]{1,0:T(8,128)S(1)}, u32[]{:S(2)}, u32[]{:S(2)}) collective-permute-start(f32[100,384]{1,0:T(8,128)} %get-tuple-element.27), channel_id=1, source_target_pairs={{0,28},{1,23},{2,30},{3,21},{4,24},{5,19},{6,26},{7,17},{8,20},{9,... | collective-permute-start | bytes 460808 | tf_op jit(solution)/shard_map/ppermute | solution.py:32
  20.5 18.9 %collective-permute-start.4 = (f32[100,384]{1,0:T(8,128)}, f32[100,384]{1,0:T(8,128)S(1)}, u32[]{:S(2)}, u32[]{:S(2)}) collective-permute-start(f32[100,384]{1,0:T(8,128)} %get-tuple-element.28), channel_id=1, source_target_pairs={{0,30},{1,9},{2,28},{3,11},{4,26},{5,13},{6,24},{7,15},{8,22},{9,1... | collective-permute-start | bytes 460808 | tf_op jit(solution)/shard_map/ppermute | solution.py:32
  35.7 11.9 %copy-start.19 = (f32[50,384]{1,0:T(8,128)}, f32[50,384]{1,0:T(8,128)S(1)}, u32[]{:S(2)}) copy-start(f32[50,384]{1,0:T(8,128)S(1)} %collective-permute-done.8.refs_7_) | copy-start | bytes 230404
  35.7 8.5 %collective-permute-start.5 = (f32[100,384]{1,0:T(8,128)}, f32[100,384]{1,0:T(8,128)S(1)}, u32[]{:S(2)}, u32[]{:S(2)}) collective-permute-start(f32[100,384]{1,0:T(8,128)} %get-tuple-element.29), channel_id=1, source_target_pairs={{0,2},{1,5},{2,0},{3,7},{4,6},{5,1},{6,4},{7,3},{8,10},{9,13},{10,... | collective-permute-start | bytes 460808 | tf_op jit(solution)/shard_map/ppermute | solution.py:32
  37.2 10.4 %copy-start.11 = (f32[100,384]{1,0:T(8,128)}, f32[100,384]{1,0:T(8,128)S(1)}, u32[]{:S(2)}) copy-start(f32[100,384]{1,0:T(8,128)S(1)} %collective-permute-done.1.refs_0_) | copy-start | bytes 460804
  37.2 10.4 %collective-permute-start.6 = (f32[100,384]{1,0:T(8,128)}, f32[100,384]{1,0:T(8,128)S(1)}, u32[]{:S(2)}, u32[]{:S(2)}) collective-permute-start(f32[100,384]{1,0:T(8,128)} %get-tuple-element.30), channel_id=1, source_target_pairs={{0,6},{1,11},{2,4},{3,9},{4,2},{5,15},{6,0},{7,13},{8,14},{9,3},{1... | collective-permute-start | bytes 460808 | tf_op jit(solution)/shard_map/ppermute | solution.py:32
  38.7 8.9 %collective-permute-start.7 = (f32[100,384]{1,0:T(8,128)}, f32[100,384]{1,0:T(8,128)S(1)}, u32[]{:S(2)}, u32[]{:S(2)}) collective-permute-start(f32[100,384]{1,0:T(8,128)} %get-tuple-element.31), channel_id=1, source_target_pairs={{0,12},{1,15},{2,14},{3,13},{4,8},{5,11},{6,10},{7,9},{8,4},{9,7},... | collective-permute-start | bytes 460808 | tf_op jit(solution)/shard_map/ppermute | solution.py:32
  52.6 1.9 %collective-permute-start.9 = (f32[256,384]{1,0:T(8,128)}, f32[256,384]{1,0:T(8,128)S(1)}, u32[]{:S(2)}, u32[]{:S(2)}) collective-permute-start(f32[256,384]{1,0:T(8,128)} %get-tuple-element.35), channel_id=1, source_target_pairs={{0,1},{1,0},{2,3},{3,2},{4,5},{5,4},{6,7},{7,6},{8,9},{9,8},{10,11... | collective-permute-start | bytes 1179656 | tf_op jit(solution)/shard_map/ppermute | solution.py:36
  66.9 1.9 %collective-permute-start.10 = (f32[256,384]{1,0:T(8,128)}, f32[256,384]{1,0:T(8,128)S(1)}, u32[]{:S(2)}, u32[]{:S(2)}) collective-permute-start(f32[256,384]{1,0:T(8,128)} %bitcast.10), channel_id=1, source_target_pairs={{0,1},{1,0},{2,3},{3,2},{4,5},{5,4},{6,7},{7,6},{8,9},{9,8},{10,11... | collective-permute-start | bytes 1179656 | tf_op jit(solution)/shard_map/ppermute | solution.py:36
  73.6 10.8 %collective-permute-start.11 = (f32[100,384]{1,0:T(8,128)}, f32[100,384]{1,0:T(8,128)S(1)}, u32[]{:S(2)}, u32[]{:S(2)}) collective-permute-start(f32[100,384]{1,0:T(8,128)} %get-tuple-element.36), channel_id=1, source_target_pairs={{0,24},{1,19},{2,26},{3,17},{4,28},{5,23},{6,30},{7,21},{8,16},{9,... | collective-permute-start | bytes 460808 | tf_op jit(solution)/shard_map/ppermute | solution.py:32
  76.7 9.9 %collective-permute-start.12 = (f32[100,384]{1,0:T(8,128)}, f32[100,384]{1,0:T(8,128)S(1)}, u32[]{:S(2)}, u32[]{:S(2)}) collective-permute-start(f32[100,384]{1,0:T(8,128)} %get-tuple-element.37), channel_id=1, source_target_pairs={{0,26},{1,21},{2,24},{3,23},{4,30},{5,17},{6,28},{7,19},{8,18},{9,... | collective-permute-start | bytes 460808 | tf_op jit(solution)/shard_map/ppermute | solution.py:32
  78.2 20.1 %collective-permute-start.13 = (f32[100,384]{1,0:T(8,128)}, f32[100,384]{1,0:T(8,128)S(1)}, u32[]{:S(2)}, u32[]{:S(2)}) collective-permute-start(f32[100,384]{1,0:T(8,128)} %get-tuple-element.38), channel_id=1, source_target_pairs={{0,28},{1,23},{2,30},{3,21},{4,24},{5,19},{6,26},{7,17},{8,20},{9,... | collective-permute-start | bytes 460808 | tf_op jit(solution)/shard_map/ppermute | solution.py:32
  81.9 16.4 %collective-permute-start.14 = (f32[100,384]{1,0:T(8,128)}, f32[100,384]{1,0:T(8,128)S(1)}, u32[]{:S(2)}, u32[]{:S(2)}) collective-permute-start(f32[100,384]{1,0:T(8,128)} %get-tuple-element.39), channel_id=1, source_target_pairs={{0,30},{1,9},{2,28},{3,11},{4,26},{5,13},{6,24},{7,15},{8,22},{9,1... | collective-permute-start | bytes 460808 | tf_op jit(solution)/shard_map/ppermute | solution.py:32
  83.1 15.2 %collective-permute-start.15 = (f32[100,384]{1,0:T(8,128)}, f32[100,384]{1,0:T(8,128)S(1)}, u32[]{:S(2)}, u32[]{:S(2)}) collective-permute-start(f32[100,384]{1,0:T(8,128)} %get-tuple-element.40), channel_id=1, source_target_pairs={{0,2},{1,5},{2,0},{3,7},{4,6},{5,1},{6,4},{7,3},{8,10},{9,13},{10,... | collective-permute-start | bytes 460808 | tf_op jit(solution)/shard_map/ppermute | solution.py:32
  84.4 19.0 %copy-start.1 = (f32[100,384]{1,0:T(8,128)}, f32[100,384]{1,0:T(8,128)S(1)}, u32[]{:S(2)}) copy-start(f32[100,384]{1,0:T(8,128)S(1)} %collective-permute-done.11.refs_0_) | copy-start | bytes 460804
  84.4 13.9 %collective-permute-start.16 = (f32[100,384]{1,0:T(8,128)}, f32[100,384]{1,0:T(8,128)S(1)}, u32[]{:S(2)}, u32[]{:S(2)}) collective-permute-start(f32[100,384]{1,0:T(8,128)} %get-tuple-element.41), channel_id=1, source_target_pairs={{0,6},{1,11},{2,4},{3,9},{4,2},{5,15},{6,0},{7,13},{8,14},{9,3},{1... | collective-permute-start | bytes 460808 | tf_op jit(solution)/shard_map/ppermute | solution.py:32
  86.6 16.8 %copy-start.2 = (f32[100,384]{1,0:T(8,128)}, f32[100,384]{1,0:T(8,128)S(1)}, u32[]{:S(2)}) copy-start(f32[100,384]{1,0:T(8,128)S(1)} %collective-permute-done.12.refs_1_) | copy-start | bytes 460804
  86.6 16.8 %collective-permute-start.17 = (f32[100,384]{1,0:T(8,128)}, f32[100,384]{1,0:T(8,128)S(1)}, u32[]{:S(2)}, u32[]{:S(2)}) collective-permute-start(f32[100,384]{1,0:T(8,128)} %get-tuple-element.42), channel_id=1, source_target_pairs={{0,12},{1,15},{2,14},{3,13},{4,8},{5,11},{6,10},{7,9},{8,4},{9,7},... | collective-permute-start | bytes 460808 | tf_op jit(solution)/shard_map/ppermute | solution.py:32
  106.3 10.0 %collective-permute-start.18 = (f32[7,50,384]{2,1,0:T(8,128)}, f32[7,50,384]{2,1,0:T(8,128)S(1)}, u32[]{:S(2)}, u32[]{:S(2)}) collective-permute-start(f32[7,50,384]{2,1,0:T(8,128)} %shard_map.68), channel_id=1, source_target_pairs={{0,1},{1,0},{2,3},{3,2},{4,5},{5,4},{6,7},{7,6},{8,9},{9,8},{10,11... | collective-permute-start | bytes 1612808 | tf_op jit(solution)/shard_map/ppermute | solution.py:36
  107.7 8.6 %collective-permute-start.19 = (f32[50,384]{1,0:T(8,128)}, f32[50,384]{1,0:T(8,128)S(1)}, u32[]{:S(2)}, u32[]{:S(2)}) collective-permute-start(f32[50,384]{1,0:T(8,128)} %get-tuple-element.43), channel_id=1, source_target_pairs={{0,16},{2,18},{4,20},{6,22},{8,24},{10,26},{12,28},{14,30},{16,0},... | collective-permute-start | bytes 230408 | tf_op jit(solution)/shard_map/ppermute | solution.py:27
  (16 other events, 55.3 us)
